TPU v7x, 32 devices: a whole 2x2x4 slice. The times are simulated.
32 devices in a mesh: dom: 8 (over y, x, core), col: 4 (over z).
Axes of the slice: x: 2, y: 2, z: 4, core: 2. Of those that a mesh axis runs over, the one named last changes fastest.
Arguments:
- features: bfloat16 [65536, 1024], P('dom', 'col')
- weight: bfloat16 [1024, 1024], P(None, 'col'), may hold values from -0.1875 to 0.1875
- out_bias: bfloat16 [1024], P('col'), may hold values from -3 to 3
- local_index: int32 [8, 64, 4], P('dom'), may hold values from 0 to 63
- local_count: int32 [8, 64], P('dom'), may hold values from 1 to 4, as said below
- local_vals: bfloat16 [8, 64, 4, 128, 128], P('dom'), may hold values from -0.1875 to 0.1875
- halo_index: int32 [8, 64, 4], P('dom'), may hold values from 0 to 31
- halo_count: int32 [8, 64], P('dom'), may hold values from 0 to 4, as said below
- halo_vals: bfloat16 [8, 64, 4, 128, 128], P('dom'), may hold values from -0.1875 to 0.1875
- send_rows: int32 [8, 8, 512], P('dom'), may hold values from 0 to 8191
- send_count: int32 [8, 8], P('dom'), may hold values from 0 to 512, as said below
Outputs:
- normalized: bfloat16 [65536, 1024], P('dom', 'col')
- channel_stats: float32 [2, 1024], P(None, 'col')
Inputs may be any that keep to these rules, and one draw needn't show every extreme that they name: `local_index`: slots k >= local_count of a row tile are not used. `local_count`: every partition has a row tile with all 4 slots used. `halo_index`: slots k >= halo_count of a row tile are not used. `halo_count`: every partition has a row tile with all 4 slots used. `send_rows`: slots s >= send_count[q, p] are not used. send_count[p, p] is 0; every partition fills all 512 slots to some other partition.
All inputs are finite; a program needn't handle non-finite values.
Results may differ from a plain program's by a relative error of at most 0.0075.
Values may be sent and summed in bfloat16 or wider, within the bound.
A program may use at most 192 MiB of HBM per device.

v0:
```python
import jax
import jax.numpy as jnp
from jax import lax
from jax.sharding import PartitionSpec as P

TILE = 128
epsilon = 1e-06


def tile_sum(sources, tile_index, tile_count, tile_vals):
    gathered = sources[tile_index]
    keep_mask = jnp.arange(tile_vals.shape[1])[None, :] < tile_count[:, None]
    masked = jnp.where(keep_mask[:, :, None, None], tile_vals, jnp.zeros_like(tile_vals))
    return jnp.einsum("tkij,tkjc->tic", masked, gathered, preferred_element_type=jnp.float32)


def on_device(
    features,
    weight,
    out_bias,
    local_index,
    local_count,
    local_vals,
    halo_index,
    halo_count,
    halo_vals,
    send_rows,
    send_count,
):
    row_count, col_width = features.shape
    peer_count = lax.axis_size("dom")
    slot_total = send_rows.shape[2]
    chosen = features[send_rows[0]]
    keep_mask = jnp.arange(slot_total)[None, :] < send_count[0][:, None]
    outgoing = jnp.where(keep_mask[:, :, None], chosen, jnp.zeros_like(chosen))
    arrived = lax.all_to_all(outgoing, "dom", split_axis=0, concat_axis=0, tiled=True)
    halo_tiles = arrived.reshape(peer_count * slot_total // TILE, TILE, col_width)
    own_tiles = features.reshape(row_count // TILE, TILE, col_width)
    summed = tile_sum(own_tiles, local_index[0], local_count[0], local_vals[0])
    summed = summed + tile_sum(halo_tiles, halo_index[0], halo_count[0], halo_vals[0])
    spread = summed.reshape(row_count, col_width).astype(jnp.bfloat16)
    node_total = row_count * peer_count
    regrouped = lax.all_to_all(spread, "col", split_axis=0, concat_axis=1, tiled=True)
    full_weight, full_bias = (
        lax.all_gather(weight, "col", axis=1, tiled=True),
        lax.all_gather(out_bias.reshape(1, col_width), "col", axis=1, tiled=True),
    )
    mixed_rows = jnp.dot(regrouped, full_weight, preferred_element_type=jnp.float32) + full_bias[
        0
    ].astype(jnp.float32)
    active = jnp.maximum(mixed_rows, 0.0)
    row_power = jnp.mean(active * active, axis=1, keepdims=True)
    scaled = active * lax.rsqrt(row_power + epsilon)
    sum_whole, square_whole = lax.psum(
        (jnp.sum(scaled, axis=0), jnp.sum(scaled * scaled, axis=0)), ("dom", "col")
    )
    normalized = lax.all_to_all(
        scaled.astype(jnp.bfloat16), "col", split_axis=1, concat_axis=0, tiled=True
    )
    column_start = lax.axis_index("col") * col_width
    sum_total = lax.dynamic_slice_in_dim(sum_whole, column_start, col_width, 0)
    square_total = lax.dynamic_slice_in_dim(square_whole, column_start, col_width, 0)
    channel_mean = sum_total / node_total
    channel_var = square_total / node_total - channel_mean * channel_mean
    return (normalized, jnp.stack([channel_mean, channel_var]))


def solution(mesh):
    in_specs = (
        P("dom", "col"),
        P(None, "col"),
        P("col"),
        P("dom", None, None),
        P("dom", None),
        P("dom", None, None, None, None),
        P("dom", None, None),
        P("dom", None),
        P("dom", None, None, None, None),
        P("dom", None, None),
        P("dom", None),
    )
    out_specs = (P("dom", "col"), P(None, "col"))
    return jax.shard_map(
        on_device, mesh=mesh, in_specs=in_specs, out_specs=out_specs, check_vma=False
    )
```

profile of v0, /device:TPU:0, one launch (start us, length us, event | category | flops | bytes accessed | tf_op | source)
XLA Modules:
  0.0 374.6 jit_solution(2426596609186330712)
XLA Ops:
  7.2 0.7 fusion.10
  7.9 0.7 iota_compare_fusion.2
  8.6 15.7 %gather_fusion.1 = bf16[4096,256]{1,0:T(8,128)(2,1)S(1)} fusion(bf16[8192,256]{1,0:T(8,128)(2,1)} %param.11, s32[4096]{0:T(1024)S(1)} %broadcast_clamp_fusion), kind=kCustom, calls=%fused_computation.1 | custom fusion | bytes 4210688 | tf_op jit(solution)/shard_map/gather | solution.py:33
  24.4 0.0 copy-start
  24.4 0.0 copy-start.1
  24.4 1.7 broadcast_select_fusion
  26.1 5.2 %all-to-all-start = ((bf16[8,512,256]{2,1,0:T(8,128)(2,1)}), bf16[8,512,256]{2,1,0:T(8,128)(2,1)S(1)}, u32[]{:S(2)}, u32[]{:S(2)}) async-start(bf16[8,512,256]{2,1,0:T(8,128)(2,1)} %broadcast_select_fusion), calls=%async_computation | async-start | bytes 4194304 | tf_op jit(solution)/shard_map/all_to_all | solution.py:36
  31.3 0.0 copy-done
  31.3 0.1 copy.19
  31.4 0.1 reshape.208
  31.5 0.0 copy-done.1
  31.5 0.1 copy.18
  31.6 0.1 reshape.192
  31.7 0.0 copy-start.2
  31.7 0.0 copy-start.3
  31.7 12.0 %gather_fusion = bf16[256,128,256]{2,1,0:T(8,128)(2,1)} fusion(bf16[64,128,256]{2,1,0:T(8,128)(2,1)} %bitcast.52, s32[1024]{0:T(1024)S(1)} %pad_clamp_fusion.1), kind=kCustom, calls=%fused_computation | custom fusion | bytes 33555456 | tf_op jit(solution)/shard_map/gather | solution.py:11
  43.7 0.0 copy-done.2
  43.7 0.1 iota_compare_fusion
  43.8 0.0 copy-done.3
  43.8 0.1 iota_compare_fusion.1
  43.9 14.0 %all-to-all-done = bf16[8,512,256]{2,1,0:T(8,128)(2,1)S(1)} async-done(((bf16[8,512,256]{2,1,0:T(8,128)(2,1)}), bf16[8,512,256]{2,1,0:T(8,128)(2,1)S(1)}, u32[]{:S(2)}, u32[]{:S(2)}) %all-to-all-start) | async-done | bytes 2097184 | tf_op jit(solution)/shard_map/all_to_all | solution.py:36
  57.9 9.7 %gather_fusion.2 = bf16[256,128,256]{2,1,0:T(8,128)(2,1)} fusion(bf16[32,128,256]{2,1,0:T(8,128)(2,1)S(1)} %bitcast.53, s32[1024]{0:T(1024)S(1)} %pad_clamp_fusion), kind=kCustom, calls=%fused_computation.2 | custom fusion | bytes 33555456 | tf_op jit(solution)/shard_map/gather | solution.py:11
  67.6 13.8 %fusion.1 = f32[64,128,256,1]{2,1,3,0:T(8,128)} fusion(bf16[64,4,128,256]{3,2,1,0:T(8,128)(2,1)} %bitcast.54, bf16[1,64,4,128,128]{4,3,2,1,0:T(8,128)(2,1)} %param.19, pred[64,4]{1,0:T(8,128)(4,1)S(1)} %iota_compare_fusion), kind=kOutput, calls=%fused_computation.6 | convolution fusion | flops 2151677952 | bytes 33554688 | tf_op jit(solution)/shard_map/tkij,tkjc->tic/dot_general | solution.py:14
  81.4 14.0 %fusion = bf16[64,128,256]{2,1,0:T(8,128)(2,1)} fusion(f32[64,128,256,1]{2,1,3,0:T(8,128)} %fusion.1, bf16[64,4,128,256]{3,2,1,0:T(8,128)(2,1)} %bitcast.55, bf16[1,64,4,128,128]{4,3,2,1,0:T(8,128)(2,1)} %param.16, pred[64,4]{1,0:T(8,128)(4,1)S(1)} %iota_compare_fusion.1), kind=kOutput, calls=%fused_computation.4 | convolution fusion | flops 2155872256 | bytes 37748992 | tf_op jit(solution)/shard_map/tkij,tkjc->tic/dot_general | solution.py:14
  95.4 0.0 copy-start.4
  95.4 6.3 %copy.20 = bf16[4,2048,256]{1,2,0:T(8,128)(2,1)} copy(bf16[4,2048,256]{2,1,0:T(8,128)(2,1)} %bitcast.56) | data formatting | bytes 8388608 | tf_op jit(solution)/shard_map/convert_element_type | solution.py:41
  101.6 4.9 %all-to-all-start.1 = ((bf16[4,2048,256]{1,2,0:T(8,128)(2,1)}), bf16[4,2048,256]{1,2,0:T(8,128)(2,1)}, u32[]{:S(2)}, u32[]{:S(2)}) async-start(bf16[4,2048,256]{1,2,0:T(8,128)(2,1)} %copy.20), calls=%async_computation.1 | async-start | bytes 8388608 | tf_op jit(solution)/shard_map/all_to_all | solution.py:43
  106.5 0.0 all-gather.4.cloned.1.call-start
  106.5 0.7 all-gather.4.cloned.1.call-update
  107.2 0.0 copy-done.4
  107.3 103.9 %all-gather.1 = bf16[4,1,256]{2,1,0:T(2,128)(2,1)S(1)} all-gather(bf16[1,1,256]{2,1,0:T(2,128)(2,1)S(1)} %reshape.220), channel_id=2, replica_groups=mesh['dom'=8,'col'=4] {'col'}, dimensions={0}, use_global_device_ids=true | all-gather | bytes 2560 | tf_op jit(solution)/shard_map/all_gather | solution.py:46
  211.2 0.0 all-gather.4.cloned.1.call-done
  211.2 19.8 %all-to-all-done.1 = bf16[4,2048,256]{1,2,0:T(8,128)(2,1)} async-done(((bf16[4,2048,256]{1,2,0:T(8,128)(2,1)}), bf16[4,2048,256]{1,2,0:T(8,128)(2,1)}, u32[]{:S(2)}, u32[]{:S(2)}) %all-to-all-start.1) | async-done | bytes 4194336 | tf_op jit(solution)/shard_map/all_to_all | solution.py:43
  231.0 7.8 %multiply_reduce_fusion.1 = (f32[2048]{0:T(1024)S(1)}, f32[2048,1024]{0,1:T(8,128)S(1)}) fusion(f32[1024]{0:T(1024)S(1)} %bitcast.61, bf16[2048,1024]{0,1:T(8,128)(2,1)} %bitcast.19, bf16[1024,1024]{1,0:T(8,128)(2,1)} %all-gather.4.cloned.1.call-done), kind=kOutput, calls=%fused_computation.10 | convolution fusion | flops 4303353856 | bytes 14692352 | tf_op jit(solution)/shard_map/dot_general | solution.py:48
  238.8 3.5 fusion.6
  242.2 4.8 %all-to-all-start.2 = ((bf16[2048,4,256]{0,2,1:T(8,128)(2,1)}), bf16[2048,4,256]{0,2,1:T(8,128)(2,1)}, u32[]{:S(2)}, u32[]{:S(2)}) async-start(bf16[2048,4,256]{0,2,1:T(8,128)(2,1)} %bitcast.57), calls=%async_computation.2 | async-start | bytes 8388608 | tf_op jit(solution)/shard_map/all_to_all | solution.py:57
  247.1 113.8 %all-reduce = (f32[1024]{0:T(1024)S(1)}, f32[1024]{0:T(1024)S(1)}) all-reduce(f32[1024]{0:T(1024)S(1)} %get-tuple-element.3, f32[1024]{0:T(1024)S(1)} %get-tuple-element.2), channel_id=1, replica_groups=mesh['dom'=8,'col'=4] {'dom','col'}, use_global_device_ids=true, to_apply=%region_4.5 | all-reduce | flops 2048 | bytes 16384 | tf_op jit(solution)/shard_map/psum | solution.py:54
  360.9 0.1 dynamic-slice_multiply_fusion
  361.0 0.6 pad_maximum_fusion
  361.5 0.0 all-to-all-done.2
  361.6 6.2 %copy.21 = bf16[4,2048,256]{2,1,0:T(8,128)(2,1)} copy(bf16[4,2048,256]{1,2,0:T(8,128)(2,1)} %bitcast.22) | data formatting | bytes 8388608 | tf_op jit(solution)/shard_map/all_to_all | solution.py:57
  (9 shorter events, 0.1 us)
Async XLA Ops:
  24.4 6.9 %copy-start = (s32[1,64,4]{1,2,0:T(4,128)S(1)}, s32[1,64,4]{1,2,0:T(4,128)}, u32[]{:S(2)}) copy-start(s32[1,64,4]{1,2,0:T(4,128)} %param.17) | copy-start | bytes 3076
  24.4 7.1 %copy-start.1 = (s32[1,64,4]{1,2,0:T(4,128)S(1)}, s32[1,64,4]{1,2,0:T(4,128)}, u32[]{:S(2)}) copy-start(s32[1,64,4]{1,2,0:T(4,128)} %param.14) | copy-start | bytes 3076
  26.1 31.8 %all-to-all-start = ((bf16[8,512,256]{2,1,0:T(8,128)(2,1)}), bf16[8,512,256]{2,1,0:T(8,128)(2,1)S(1)}, u32[]{:S(2)}, u32[]{:S(2)}) async-start(bf16[8,512,256]{2,1,0:T(8,128)(2,1)} %broadcast_select_fusion), calls=%async_computation | async-start | bytes 4194304 | tf_op jit(solution)/shard_map/all_to_all | solution.py:36
  31.7 12.0 %copy-start.2 = (s32[1,64]{1,0:T(1,128)S(1)}, s32[1,64]{1,0:T(1,128)}, u32[]{:S(2)}) copy-start(s32[1,64]{1,0:T(1,128)} %param.18) | copy-start | bytes 772
  31.7 12.1 %copy-start.3 = (s32[1,64]{1,0:T(1,128)S(1)}, s32[1,64]{1,0:T(1,128)}, u32[]{:S(2)}) copy-start(s32[1,64]{1,0:T(1,128)} %param.15) | copy-start | bytes 772
  95.4 11.9 %copy-start.4 = (bf16[256]{0:T(256)(128)(2,1)S(1)}, bf16[256]{0:T(256)(128)(2,1)}, u32[]{:S(2)}) copy-start(bf16[256]{0:T(256)(128)(2,1)} %param.13) | copy-start | bytes 1540
  101.6 129.3 %all-to-all-start.1 = ((bf16[4,2048,256]{1,2,0:T(8,128)(2,1)}), bf16[4,2048,256]{1,2,0:T(8,128)(2,1)}, u32[]{:S(2)}, u32[]{:S(2)}) async-start(bf16[4,2048,256]{1,2,0:T(8,128)(2,1)} %copy.20), calls=%async_computation.1 | async-start | bytes 8388608 | tf_op jit(solution)/shard_map/all_to_all | solution.py:43
  106.5 104.7 %all-gather.4.cloned.1.call-start = ((), (), s32[]{:S(2)}) async-start(), calls=%async_computation.3 | async-start | bytes 2621440 | tf_op jit(solution)/shard_map/all_gather | solution.py:45
  242.2 119.3 %all-to-all-start.2 = ((bf16[2048,4,256]{0,2,1:T(8,128)(2,1)}), bf16[2048,4,256]{0,2,1:T(8,128)(2,1)}, u32[]{:S(2)}, u32[]{:S(2)}) async-start(bf16[2048,4,256]{0,2,1:T(8,128)(2,1)} %bitcast.57), calls=%async_computation.2 | async-start | bytes 8388608 | tf_op jit(solution)/shard_map/all_to_all | solution.py:57
Sparse Core Ops, SparseCore 0:
  108.9 94.7 all-gather.3
where the time goes:
time: 375 us
  blocking collectives  218 us (58%)
  local copies, waits for them, and re-layouts  50.3 us (13%)
  matrix products  35.5 us (9%)
  waiting for transfers between devices  34.5 us (9%)
  starting transfers between devices  14.9 us (4%)
  between operations  14.2 us (4%)
  other arithmetic  7.48 us (2%)
    psum x1, blocking collectives, on_device(): lax.psum((jnp.sum(scaled, axis=0), jnp.sum(scaled * scaled, axis=0)), ('d...  114 us
    all_gather x1, blocking collectives, on_device(): lax.all_gather(out_bias.reshape(1, col_width), 'col', axis=1, tiled=True)  104 us
    dot_general x2, matrix products, tile_sum(): jnp.einsum('tkij,tkjc->tic', masked, gathered, preferred_element_type=jnp...  27.7 us
    gather x2, local copies, waits for them, and re-layouts, tile_sum(): gathered = sources[tile_index]  21.7 us
    all_to_all x1, waiting for transfers between devices, on_device(): lax.all_to_all(spread, 'col', split_axis=0, concat_axis=1, tiled=True)  19.8 us
    gather x1, local copies, waits for them, and re-layouts, on_device(): chosen = features[send_rows[0]]  15.7 us
    all_to_all x1, waiting for transfers between devices, on_device(): lax.all_to_all(outgoing, 'dom', split_axis=0, concat_axis=0, tiled=True)  14 us
    dot_general x1, matrix products, on_device(): jnp.dot(regrouped, full_weight, preferred_element_type=jnp.float32)  7.76 us
  transfers between devices with their start and end apart: 4, of which 2 were waited for; matrix products, arithmetic and copies ran while one was open for 4% of the time, Pallas kernels for 0%

commit v1 on v0

--- a/solution.py
+++ b/solution.py
@@ -52,7 +52,7 @@
     row_power = jnp.mean(active * active, axis=1, keepdims=True)
     scaled = active * lax.rsqrt(row_power + epsilon)
     sum_whole, square_whole = lax.psum(
-        (jnp.sum(scaled, axis=0), jnp.sum(scaled * scaled, axis=0)), ("dom", "col")
+        lax.psum((jnp.sum(scaled, axis=0), jnp.sum(scaled * scaled, axis=0)), "col"), "dom"
     )
     normalized = lax.all_to_all(
         scaled.astype(jnp.bfloat16), "col", split_axis=1, concat_axis=0, tiled=True

time: 375 us -> 367 us (0.979)
  the two profiles are of different devices: /device:TPU:0 before, /device:TPU:20 now
where the time goes in v1:
time: 367 us
  blocking collectives  232 us (63%)
  local copies, waits for them, and re-layouts  50.2 us (14%)
  matrix products  35.5 us (10%)
  starting transfers between devices  14.3 us (4%)
  between operations  14.2 us (4%)
  waiting for transfers between devices  13.3 us (4%)
  other arithmetic  7.49 us (2%)
    all_gather x1, blocking collectives, on_device(): lax.all_gather(out_bias.reshape(1, col_width), 'col', axis=1, tiled=True)  125 us
    psum x1, blocking collectives, on_device(): lax.psum((jnp.sum(scaled, axis=0), jnp.sum(scaled * scaled, axis=0)), 'col')  93.3 us
    dot_general x2, matrix products, tile_sum(): jnp.einsum('tkij,tkjc->tic', masked, gathered, preferred_element_type=jnp...  27.7 us
    gather x2, local copies, waits for them, and re-layouts, tile_sum(): gathered = sources[tile_index]  21.6 us
    gather x1, local copies, waits for them, and re-layouts, on_device(): chosen = features[send_rows[0]]  15.7 us
    psum x1, blocking collectives, on_device(): lax.psum(lax.psum((jnp.sum(scaled, axis=0), jnp.sum(scaled * scaled, axis...  13.4 us
    all_to_all x1, waiting for transfers between devices, on_device(): lax.all_to_all(outgoing, 'dom', split_axis=0, concat_axis=0, tiled=True)  12.5 us
    dot_general x1, matrix products, on_device(): jnp.dot(regrouped, full_weight, preferred_element_type=jnp.float32)  7.77 us
  transfers between devices with their start and end apart: 4, of which 1 were waited for; matrix products, arithmetic and copies ran while one was open for 4% of the time, Pallas kernels for 0%

profile of v1, /device:TPU:20, one launch (start us, length us, event | category | flops | bytes accessed | tf_op | source)
XLA Modules:
  0.0 366.7 jit_solution(13052043358232617304)
XLA Ops:
  7.2 0.7 fusion.10
  7.9 0.7 iota_compare_fusion.2
  8.6 15.7 %gather_fusion.1 = bf16[4096,256]{1,0:T(8,128)(2,1)S(1)} fusion(bf16[8192,256]{1,0:T(8,128)(2,1)} %param.11, s32[4096]{0:T(1024)S(1)} %broadcast_clamp_fusion), kind=kCustom, calls=%fused_computation.1 | custom fusion | bytes 4210688 | tf_op jit(solution)/shard_map/gather | solution.py:33
  24.4 0.0 copy-start
  24.4 0.0 copy-start.1
  24.4 1.7 broadcast_select_fusion
  26.1 4.2 %all-to-all-start = ((bf16[8,512,256]{2,1,0:T(8,128)(2,1)}), bf16[8,512,256]{2,1,0:T(8,128)(2,1)S(1)}, u32[]{:S(2)}, u32[]{:S(2)}) async-start(bf16[8,512,256]{2,1,0:T(8,128)(2,1)} %broadcast_select_fusion), calls=%async_computation | async-start | bytes 4194304 | tf_op jit(solution)/shard_map/all_to_all | solution.py:36
  30.3 0.0 copy-done
  30.3 0.1 copy.19
  30.4 0.1 reshape.208
  30.5 0.0 copy-done.1
  30.5 0.1 copy.18
  30.6 0.1 reshape.192
  30.7 0.0 copy-start.2
  30.8 0.0 copy-start.3
  30.8 12.0 %gather_fusion = bf16[256,128,256]{2,1,0:T(8,128)(2,1)} fusion(bf16[64,128,256]{2,1,0:T(8,128)(2,1)} %bitcast.52, s32[1024]{0:T(1024)S(1)} %pad_clamp_fusion.1), kind=kCustom, calls=%fused_computation | custom fusion | bytes 33555456 | tf_op jit(solution)/shard_map/gather | solution.py:11
  42.7 0.0 copy-done.2
  42.7 0.1 iota_compare_fusion
  42.8 0.0 copy-done.3
  42.8 0.1 iota_compare_fusion.1
  42.9 12.5 %all-to-all-done = bf16[8,512,256]{2,1,0:T(8,128)(2,1)S(1)} async-done(((bf16[8,512,256]{2,1,0:T(8,128)(2,1)}), bf16[8,512,256]{2,1,0:T(8,128)(2,1)S(1)}, u32[]{:S(2)}, u32[]{:S(2)}) %all-to-all-start) | async-done | bytes 2097184 | tf_op jit(solution)/shard_map/all_to_all | solution.py:36
  55.4 9.7 %gather_fusion.2 = bf16[256,128,256]{2,1,0:T(8,128)(2,1)} fusion(bf16[32,128,256]{2,1,0:T(8,128)(2,1)S(1)} %bitcast.53, s32[1024]{0:T(1024)S(1)} %pad_clamp_fusion), kind=kCustom, calls=%fused_computation.2 | custom fusion | bytes 33555456 | tf_op jit(solution)/shard_map/gather | solution.py:11
  65.1 13.8 %fusion.1 = f32[64,128,256,1]{2,1,3,0:T(8,128)} fusion(bf16[64,4,128,256]{3,2,1,0:T(8,128)(2,1)} %bitcast.54, bf16[1,64,4,128,128]{4,3,2,1,0:T(8,128)(2,1)} %param.19, pred[64,4]{1,0:T(8,128)(4,1)S(1)} %iota_compare_fusion), kind=kOutput, calls=%fused_computation.6 | convolution fusion | flops 2151677952 | bytes 33554688 | tf_op jit(solution)/shard_map/tkij,tkjc->tic/dot_general | solution.py:14
  78.9 14.0 %fusion = bf16[64,128,256]{2,1,0:T(8,128)(2,1)} fusion(f32[64,128,256,1]{2,1,3,0:T(8,128)} %fusion.1, bf16[64,4,128,256]{3,2,1,0:T(8,128)(2,1)} %bitcast.55, bf16[1,64,4,128,128]{4,3,2,1,0:T(8,128)(2,1)} %param.16, pred[64,4]{1,0:T(8,128)(4,1)S(1)} %iota_compare_fusion.1), kind=kOutput, calls=%fused_computation.4 | convolution fusion | flops 2155872256 | bytes 37748992 | tf_op jit(solution)/shard_map/tkij,tkjc->tic/dot_general | solution.py:14
  92.9 0.0 copy-start.4
  92.9 6.3 %copy.20 = bf16[4,2048,256]{1,2,0:T(8,128)(2,1)} copy(bf16[4,2048,256]{2,1,0:T(8,128)(2,1)} %bitcast.56) | data formatting | bytes 8388608 | tf_op jit(solution)/shard_map/convert_element_type | solution.py:41
  99.1 5.2 %all-to-all-start.1 = ((bf16[4,2048,256]{1,2,0:T(8,128)(2,1)}), bf16[4,2048,256]{1,2,0:T(8,128)(2,1)}, u32[]{:S(2)}, u32[]{:S(2)}) async-start(bf16[4,2048,256]{1,2,0:T(8,128)(2,1)} %copy.20), calls=%async_computation.1 | async-start | bytes 8388608 | tf_op jit(solution)/shard_map/all_to_all | solution.py:43
  104.3 0.0 all-gather.4.cloned.1.call-start
  104.3 0.7 all-gather.4.cloned.1.call-update
  105.1 0.0 copy-done.4
  105.1 125.0 %all-gather.1 = bf16[4,1,256]{2,1,0:T(2,128)(2,1)S(1)} all-gather(bf16[1,1,256]{2,1,0:T(2,128)(2,1)S(1)} %reshape.220), channel_id=2, replica_groups=mesh['dom'=8,'col'=4] {'col'}, dimensions={0}, use_global_device_ids=true | all-gather | bytes 2560 | tf_op jit(solution)/shard_map/all_gather | solution.py:46
  230.1 0.0 all-gather.4.cloned.1.call-done
  230.1 0.0 all-to-all-done.1
  230.1 7.8 %multiply_reduce_fusion.1 = (f32[2048]{0:T(1024)S(1)}, f32[2048,1024]{0,1:T(8,128)S(1)}) fusion(f32[1024]{0:T(1024)S(1)} %bitcast.61, bf16[2048,1024]{0,1:T(8,128)(2,1)} %bitcast.19, bf16[1024,1024]{1,0:T(8,128)(2,1)} %all-gather.4.cloned.1.call-done), kind=kOutput, calls=%fused_computation.10 | convolution fusion | flops 4303353856 | bytes 14692352 | tf_op jit(solution)/shard_map/dot_general | solution.py:48
  237.9 3.5 fusion.6
  241.4 4.9 %all-to-all-start.2 = ((bf16[2048,4,256]{0,2,1:T(8,128)(2,1)}), bf16[2048,4,256]{0,2,1:T(8,128)(2,1)}, u32[]{:S(2)}, u32[]{:S(2)}) async-start(bf16[2048,4,256]{0,2,1:T(8,128)(2,1)} %bitcast.57), calls=%async_computation.2 | async-start | bytes 8388608 | tf_op jit(solution)/shard_map/all_to_all | solution.py:57
  246.2 93.3 %all-reduce.1 = (f32[1024]{0:T(1024)S(1)}, f32[1024]{0:T(1024)S(1)}) all-reduce(f32[1024]{0:T(1024)S(1)} %get-tuple-element.3, f32[1024]{0:T(1024)S(1)} %get-tuple-element.2), channel_id=1, replica_groups=mesh['dom'=8,'col'=4] {'col'}, use_global_device_ids=true, to_apply=%region_5.6 | all-reduce | flops 2048 | bytes 16384 | tf_op jit(solution)/shard_map/psum | solution.py:55
  339.5 13.4 %all-reduce = (f32[1024]{0:T(1024)S(1)}, f32[1024]{0:T(1024)S(1)}) all-reduce(f32[1024]{0:T(1024)S(1)} %get-tuple-element.6, f32[1024]{0:T(1024)S(1)} %get-tuple-element.7), channel_id=1, replica_groups=mesh['dom'=8,'col'=4] {'dom'}, use_global_device_ids=true, to_apply=%region_6.7 | all-reduce | flops 2048 | bytes 16384 | tf_op jit(solution)/shard_map/psum | solution.py:54
  352.9 0.1 dynamic-slice_multiply_fusion
  353.0 0.6 pad_maximum_fusion
  353.6 0.0 all-to-all-done.2
  353.6 6.2 %copy.21 = bf16[4,2048,256]{2,1,0:T(8,128)(2,1)} copy(bf16[4,2048,256]{1,2,0:T(8,128)(2,1)} %bitcast.22) | data formatting | bytes 8388608 | tf_op jit(solution)/shard_map/all_to_all | solution.py:57
  (9 shorter events, 0.1 us)
Async XLA Ops:
  24.4 5.9 %copy-start = (s32[1,64,4]{1,2,0:T(4,128)S(1)}, s32[1,64,4]{1,2,0:T(4,128)}, u32[]{:S(2)}) copy-start(s32[1,64,4]{1,2,0:T(4,128)} %param.17) | copy-start | bytes 3076
  24.4 6.1 %copy-start.1 = (s32[1,64,4]{1,2,0:T(4,128)S(1)}, s32[1,64,4]{1,2,0:T(4,128)}, u32[]{:S(2)}) copy-start(s32[1,64,4]{1,2,0:T(4,128)} %param.14) | copy-start | bytes 3076
  26.1 29.4 %all-to-all-start = ((bf16[8,512,256]{2,1,0:T(8,128)(2,1)}), bf16[8,512,256]{2,1,0:T(8,128)(2,1)S(1)}, u32[]{:S(2)}, u32[]{:S(2)}) async-start(bf16[8,512,256]{2,1,0:T(8,128)(2,1)} %broadcast_select_fusion), calls=%async_computation | async-start | bytes 4194304 | tf_op jit(solution)/shard_map/all_to_all | solution.py:36
  30.7 12.0 %copy-start.2 = (s32[1,64]{1,0:T(1,128)S(1)}, s32[1,64]{1,0:T(1,128)}, u32[]{:S(2)}) copy-start(s32[1,64]{1,0:T(1,128)} %param.18) | copy-start | bytes 772
  30.8 12.1 %copy-start.3 = (s32[1,64]{1,0:T(1,128)S(1)}, s32[1,64]{1,0:T(1,128)}, u32[]{:S(2)}) copy-start(s32[1,64]{1,0:T(1,128)} %param.15) | copy-start | bytes 772
  92.9 12.2 %copy-start.4 = (bf16[256]{0:T(256)(128)(2,1)S(1)}, bf16[256]{0:T(256)(128)(2,1)}, u32[]{:S(2)}) copy-start(bf16[256]{0:T(256)(128)(2,1)} %param.13) | copy-start | bytes 1540
  99.1 130.9 %all-to-all-start.1 = ((bf16[4,2048,256]{1,2,0:T(8,128)(2,1)}), bf16[4,2048,256]{1,2,0:T(8,128)(2,1)}, u32[]{:S(2)}, u32[]{:S(2)}) async-start(bf16[4,2048,256]{1,2,0:T(8,128)(2,1)} %copy.20), calls=%async_computation.1 | async-start | bytes 8388608 | tf_op jit(solution)/shard_map/all_to_all | solution.py:43
  104.3 125.7 %all-gather.4.cloned.1.call-start = ((), (), s32[]{:S(2)}) async-start(), calls=%async_computation.3 | async-start | bytes 2621440 | tf_op jit(solution)/shard_map/all_gather | solution.py:45
  241.4 112.3 %all-to-all-start.2 = ((bf16[2048,4,256]{0,2,1:T(8,128)(2,1)}), bf16[2048,4,256]{0,2,1:T(8,128)(2,1)}, u32[]{:S(2)}, u32[]{:S(2)}) async-start(bf16[2048,4,256]{0,2,1:T(8,128)(2,1)} %bitcast.57), calls=%async_computation.2 | async-start | bytes 8388608 | tf_op jit(solution)/shard_map/all_to_all | solution.py:57
Sparse Core Ops, SparseCore 0:
  106.7 106.2 all-gather.3
